TPU v7x, 32 devices: a whole 2x2x4 slice. The times are simulated.
32 devices in a mesh: rep: 16 (over z, y, core), tp: 2 (over x).
Axes of the slice: x: 2, y: 2, z: 4, core: 2. Of those that a mesh axis runs over, the one named last changes fastest.
Arguments:
- activations: bfloat16 [8192, 6144], P('rep', 'tp'), may hold values from -6 to 6
- norm_gain: float32 [6144], replicated, may hold values from 0.5 to 1.5
- query_gain: float32 [128], replicated, may hold values from 0.5 to 18
- key_gain: float32 [128], replicated, may hold values from 0.5 to 18
- project_in: bfloat16 [6144, 24, 384], P('rep', 'tp'), may hold values from -1 to 1
- project_out: bfloat16 [6144, 3072], P('rep', 'tp'), may hold values from -1 to 1
Outputs:
- attended: bfloat16 [8192, 6144], P('rep', 'tp')
- weight_norms: float32 [2], replicated
All inputs are finite; a program needn't handle non-finite values.
Results may differ from a plain program's by a relative error of at most 0.018.
The roundings to bfloat16 on the way count: a program that leaves them out, or rounds other values in their place, can miss the bound.
Values may be sent and summed in bfloat16 or wider, within the bound.
A program may use at most 192 MiB of HBM per device.

v0:
```python
import functools
import math
import jax
import jax.numpy as jnp
from jax import lax
from jax.sharding import PartitionSpec as P

D = 6144
HEADS = 24
HEAD_DIM = 128
PATCHES = 256


def layer_norm(values, gain):
    average = jnp.mean(values, -1, keepdims=True)
    centred = values - average
    variance = jnp.mean(centred * centred, -1, keepdims=True)
    return centred * lax.rsqrt(variance + 1e-06) * gain


def heads_mixed(projected, query_gain, key_gain, head_dim):
    tok_rows, width = projected.shape
    heads = width // (3 * head_dim)
    projected = projected.reshape(tok_rows // PATCHES, PATCHES, heads, 3 * head_dim)
    queries = layer_norm(projected[..., :head_dim], query_gain).astype(jnp.bfloat16)
    keys_normed = layer_norm(projected[..., head_dim : 2 * head_dim], key_gain).astype(jnp.bfloat16)
    values = projected[..., 2 * head_dim :].astype(jnp.bfloat16)
    scores = jnp.einsum(
        "iphd,iqhd->ihpq", queries, keys_normed, preferred_element_type=jnp.float32
    ) / math.sqrt(head_dim)
    probabilities = jax.nn.softmax(scores, axis=-1).astype(jnp.bfloat16)
    mixed = jnp.einsum("ihpq,iqhd->iphd", probabilities, values, preferred_element_type=jnp.float32)
    return mixed.astype(jnp.bfloat16).reshape(tok_rows, heads * head_dim)


def chunk_count(size, wanted):
    while size % wanted:
        wanted -= 1
    return wanted


def shards(n_rep, n_tp, activations, norm_gain, query_gain, key_gain, project_in, project_out):
    me = lax.axis_index("tp")
    swap = [(0, 1), (1, 0)]
    local_rows, local_heads, head_width = project_in.shape
    head_dim = head_width // 3
    n_in = chunk_count(local_heads, 3)
    step = local_heads // n_in
    pieces = []
    for j in range(n_in):
        part = project_in[:, j * step : (j + 1) * step].reshape(local_rows, step * head_width)
        pieces.append(lax.all_gather(part, "rep", axis=0, tiled=True))
    out_rows, out_depth = project_out.shape
    n_out = chunk_count(out_rows // 128, 3) if out_rows % 128 == 0 else 1
    span = out_rows // n_out
    out_pieces = []
    for j in range(n_out):
        part = project_out[j * span : (j + 1) * span]
        out_pieces.append(lax.all_gather(part, "rep", axis=0, tiled=True))
    local_in = jnp.sum(jnp.square(project_in.astype(jnp.float32)))
    local_out = jnp.sum(jnp.square(project_out.astype(jnp.float32)))
    totals = lax.psum(jnp.stack([local_in, local_out]), ("rep", "tp"))
    if n_tp == 2:
        other = lax.ppermute(activations, "tp", swap)
        other, totals = lax.optimization_barrier((other, totals))
        first = jnp.where(me == 0, activations, other)
        second = jnp.where(me == 0, other, activations)
        gathered_rows = jnp.concatenate([first, second], axis=1)
    else:
        gathered_rows = lax.all_gather(activations, "tp", axis=1, tiled=True)
    normed = layer_norm(gathered_rows.astype(jnp.float32), norm_gain).astype(jnp.bfloat16)
    mixed = []
    for piece in pieces:
        projected = jnp.dot(normed, piece, preferred_element_type=jnp.float32)
        mixed.append(heads_mixed(projected, query_gain, key_gain, head_dim))
    mixed = jnp.concatenate(mixed, axis=1)

    def product(rows):
        total = lax.dot_general(
            mixed, rows, (((1,), (1,)), ((), ())), preferred_element_type=jnp.float32
        )
        return total.astype(jnp.bfloat16)

    sums = []
    for piece in out_pieces:
        if n_tp == 2:
            half = piece.shape[0] // 2
            sent = product(lax.dynamic_slice_in_dim(piece, (1 - me) * half, half, 0))
            arrived = lax.ppermute(sent, "tp", swap)
            kept = product(lax.dynamic_slice_in_dim(piece, me * half, half, 0))
            total = kept.astype(jnp.float32) + arrived.astype(jnp.float32)
            sums.append(total.astype(jnp.bfloat16))
        else:
            sums.append(lax.psum_scatter(product(piece), "tp", scatter_dimension=1, tiled=True))
    owners = n_rep // n_tp
    blocks = [sums[j][:, r * span : (r + 1) * span] for r in range(owners) for j in range(n_out)]
    attended = jnp.concatenate(blocks, axis=1)
    fans = jnp.array([3 * HEADS * HEAD_DIM, D], jnp.float32)
    return (attended, jnp.sqrt(totals / fans))


def solution(mesh):
    in_specs = (P("rep", "tp"), P(), P(), P(), P("rep", "tp", None), P("rep", "tp"))
    out_specs = (P("rep", "tp"), P())
    body = functools.partial(shards, mesh.shape["rep"], mesh.shape["tp"])
    return jax.shard_map(body, mesh=mesh, in_specs=in_specs, out_specs=out_specs, check_vma=False)
```

profile of v0, /device:TPU:0, one launch (start us, length us, event | category | flops | bytes accessed | tf_op | source)
XLA Modules:
  0.0 543.6 jit_solution(12540614699131464713)
XLA Ops:
  7.2 2.4 fusion.113
  9.6 1.5 copy.45
  11.2 1.5 copy.48
  12.7 1.5 copy.42
  14.3 2.4 fusion.114
  17.4 3.0 collective-permute-start
  20.4 2.6 multiply_reduce_fusion.1
  23.0 2.4 multiply_reduce_fusion
  25.4 1.4 pad_maximum_fusion.1
  26.8 98.2 %psum.7 = f32[2]{0:T(128)S(1)} all-reduce(f32[2]{0:T(128)S(1)} %pad_maximum_fusion.1), channel_id=1, replica_groups=mesh['rep'=16,'tp'=2] {'rep','tp'}, use_global_device_ids=true, to_apply=%region_2.0 | all-reduce | flops 2 | bytes 16 | tf_op jit(solution)/shard_map/psum | solution.py:62
  125.0 3.3 broadcast_select_fusion.1
  128.3 0.9 convert_reduce_fusion
  129.2 0.7 copy-done
  129.9 4.1 fusion.5
  134.1 16.9 %fusion.109 = f32[512,1536]{1,0:T(8,128)} fusion(bf16[6144,1536]{0,1:T(8,128)(2,1)} %all-gather.9.cloned.1.call-done, f32[6144]{0:T(1024)S(1)} %copy-done.12, f32[512]{0:T(512)S(1)} %add_rsqrt_fusion.6, f32[512]{0:T(512)S(1)} %broadcast_multiply_fusion.6, bf16[512,3072]{1,0:T(8,128)(2,1)} %copy-done, bf16[512,3072]{1,0:T(8,128)(2,1)S(1)} %get-tuple-element.12), kind=kOutput, calls=%fused_computation.164 | convolution fusion | flops 9688842240 | bytes 28340224 | tf_op jit(solution)/shard_map/dot_general | solution.py:74
  151.0 4.8 reshape.128
  155.8 58.2 %all-gather.11.cloned.1.call-done = bf16[6144,1536]{0,1:T(8,128)(2,1)} async-done(((bf16[384,1536]{0,1:T(8,128)(2,1)}), bf16[6144,1536]{0,1:T(8,128)(2,1)}) %all-gather.11.cloned.1.call-update) | async-done | bytes 18874384 | tf_op jit(solution)/shard_map/all_gather | solution.py:52
  214.0 17.3 %fusion.107 = f32[512,1536]{1,0:T(8,128)} fusion(bf16[6144,1536]{0,1:T(8,128)(2,1)} %all-gather.11.cloned.1.call-done, f32[6144]{0:T(1024)S(1)} %copy-done.12, f32[512]{0:T(512)S(1)} %add_rsqrt_fusion.6, f32[512]{0:T(512)S(1)} %broadcast_multiply_fusion.6, bf16[512,3072]{1,0:T(8,128)(2,1)} %copy-done, bf16[512,3072]{1,0:T(8,128)(2,1)S(1)} %get-tuple-element.12), kind=kOutput, calls=%fused_computation.163 | convolution fusion | flops 9688842240 | bytes 28340224 | tf_op jit(solution)/shard_map/dot_general | solution.py:74
  231.3 4.9 reshape.131
  236.2 6.6 %slice_reduce_fusion.1 = (f32[2,256,4]{2,1,0:T(8,128)}, f32[2,256,4]{2,1,0:T(8,128)}, f32[2,256,4,128]{3,2,1,0:T(4,128)}, f32[2,256,4,128]{3,2,1,0:T(4,128)}, f3...) fusion(f32[2,256,4,384]{3,2,1,0:T(4,128)} %reshape.131, ...), kind=kLoop, calls=%fused_computation.158 | loop fusion | flops 1040384 | bytes 8421376 | tf_op jit(solution)/shard_map/reduce_sum | solution.py:15
  242.8 2.2 slice.165
  245.1 2.2 slice.162
  247.3 1.1 copy.55
  248.3 1.1 copy.56
  249.4 2.1 copy.59
  251.5 1.9 multiply_reduce_fusion.6
  253.4 1.9 multiply_reduce_fusion.5
  255.3 2.9 fusion.55
  258.2 1.3 copy-done.4
  260.1 3.5 fusion.49
  263.6 2.1 copy.38
  265.7 1.1 copy.53
  266.9 2.1 copy.58
  269.0 1.9 multiply_reduce_fusion.8
  270.9 1.9 multiply_reduce_fusion.7
  272.8 2.7 fusion.54
  275.5 1.3 copy-done.5
  277.4 3.4 fusion.48
  280.8 2.1 copy.32
  282.9 31.5 %all-gather.7.cloned.1.call-done = bf16[6144,1536]{0,1:T(8,128)(2,1)} async-done(((bf16[384,1536]{0,1:T(8,128)(2,1)}), bf16[6144,1536]{0,1:T(8,128)(2,1)}) %all-gather.7.cloned.1.call-update) | async-done | bytes 18874384 | tf_op jit(solution)/shard_map/all_gather | solution.py:52
  314.4 16.6 %fusion.111 = f32[512,1536]{1,0:T(8,128)} fusion(bf16[6144,1536]{0,1:T(8,128)(2,1)} %all-gather.7.cloned.1.call-done, f32[6144]{0:T(1024)S(1)} %copy-done.12, f32[512]{0:T(512)S(1)} %add_rsqrt_fusion.6, f32[512]{0:T(512)S(1)} %broadcast_multiply_fusion.6, bf16[512,3072]{1,0:T(8,128)(2,1)} %copy-done, bf16[512,3072]{1,0:T(8,128)(2,1)S(1)} %get-tuple-element.12), kind=kOutput, calls=%fused_computation.165 | convolution fusion | flops 9688842240 | bytes 28340224 | tf_op jit(solution)/shard_map/dot_general | solution.py:74
  331.0 3.2 reshape.125
  334.2 1.0 slice.159
  335.2 3.1 slice_reduce_fusion.5
  338.3 1.2 copy.52
  339.7 1.3 copy.57
  341.0 2.7 multiply_reduce_fusion.9
  343.7 1.3 fusion.53
  345.0 1.3 copy-done.6
  347.0 2.4 fusion.47
  350.5 27.4 %all-gather.13.cloned.1.call-done = bf16[2048,1536]{1,0:T(8,128)(2,1)} async-done(((bf16[128,1536]{1,0:T(8,128)(2,1)}), bf16[2048,1536]{1,0:T(8,128)(2,1)}) %all-gather.13.cloned.1.call-update) | async-done | bytes 6291472 | tf_op jit(solution)/shard_map/all_gather | solution.py:59
  377.9 4.7 fusion.26
  382.6 1.5 collective-permute-start.1
  384.6 55.6 %all-gather.15.cloned.1.call-done = bf16[2048,1536]{1,0:T(8,128)(2,1)} async-done(((bf16[128,1536]{1,0:T(8,128)(2,1)}), bf16[2048,1536]{1,0:T(8,128)(2,1)}) %all-gather.15.cloned.1.call-update) | async-done | bytes 6291472 | tf_op jit(solution)/shard_map/all_gather | solution.py:59
  440.2 4.7 fusion.32
  444.9 1.5 collective-permute-start.2
  446.4 56.1 %all-gather.17.cloned.1.call-done = bf16[2048,1536]{1,0:T(8,128)(2,1)} async-done(((bf16[128,1536]{1,0:T(8,128)(2,1)}), bf16[2048,1536]{1,0:T(8,128)(2,1)}) %all-gather.17.cloned.1.call-update) | async-done | bytes 6291472 | tf_op jit(solution)/shard_map/all_gather | solution.py:59
  502.5 3.9 fusion.38
  506.3 1.5 collective-permute-start.3
  507.9 3.7 add_convert_fusion.2
  511.7 3.2 add_convert_fusion.1
  515.0 16.7 %collective-permute-done.3 = bf16[512,1024]{1,0:T(8,128)(2,1)S(1)} collective-permute-done((bf16[512,1024]{1,0:T(8,128)(2,1)S(1)}, bf16[512,1024]{1,0:T(8,128)(2,1)S(1)}, u32[]{:S(2)}, u32[]{:S(2)}) %collective-permute-start.3) | collective-permute-done | bytes 1048608 | tf_op jit(solution)/shard_map/ppermute | solution.py:89
  531.7 1.8 add_convert_fusion
  534.8 1.7 copy-done.9
  (97 shorter events, 5.8 us)
Async XLA Ops:
  7.2 126.9 %all-gather.9.cloned.1.call-start = ((), (), s32[]{:S(2)}) async-start(), calls=%async_computation.1 | async-start | bytes 20054016 | tf_op jit(solution)/shard_map/all_gather | solution.py:52
  11.1 202.9 %all-gather.11.cloned.1.call-start = ((), (), s32[]{:S(2)}) async-start(), calls=%async_computation.2 | async-start | bytes 20054016 | tf_op jit(solution)/shard_map/all_gather | solution.py:52
  12.7 301.7 %all-gather.7.cloned.1.call-start = ((), (), s32[]{:S(2)}) async-start(), calls=%async_computation | async-start | bytes 20054016 | tf_op jit(solution)/shard_map/all_gather | solution.py:52
  14.2 8.8 %copy-start.1 = (bf16[384,12,384]{2,0,1:T(8,128)(2,1)S(1)}, bf16[384,12,384]{2,0,1:T(8,128)(2,1)}, u32[]{:S(2)}) copy-start(bf16[384,12,384]{2,0,1:T(8,128)(2,1)} %param.11) | copy-start | bytes 10616836
  14.2 363.7 %all-gather.13.cloned.1.call-start = ((), (), s32[]{:S(2)}) async-start(), calls=%async_computation.3 | async-start | bytes 6684672 | tf_op jit(solution)/shard_map/all_gather | solution.py:59
  16.7 423.5 %all-gather.15.cloned.1.call-start = ((), (), s32[]{:S(2)}) async-start(), calls=%async_computation.4 | async-start | bytes 6684672 | tf_op jit(solution)/shard_map/all_gather | solution.py:59
  17.3 485.1 %all-gather.17.cloned.1.call-start = ((), (), s32[]{:S(2)}) async-start(), calls=%async_computation.5 | async-start | bytes 6684672 | tf_op jit(solution)/shard_map/all_gather | solution.py:59
  17.4 107.6 %collective-permute-start = (bf16[512,3072]{1,0:T(8,128)(2,1)}, bf16[512,3072]{1,0:T(8,128)(2,1)}, u32[]{:S(2)}, u32[]{:S(2)}) collective-permute-start(bf16[512,3072]{1,0:T(8,128)(2,1)} %param.7), channel_id=1, source_target_pairs={{0,1},{1,0},{2,3},{3,2},{4,5},{5,4},{6,7},{7,6},{8,9},{9,8},{10,11... | collective-permute-start | bytes 9437192 | tf_op jit(solution)/shard_map/ppermute | solution.py:64
  128.3 1.7 copy-start
  129.9 4.2 copy-start.12
  242.8 12.4 %copy-start.10 = (f32[128]{0:T(128)S(1)}, f32[128]{0:T(128)}, u32[]{:S(2)}) copy-start(f32[128]{0:T(128)} %param.10) | copy-start | bytes 1540
  242.8 12.5 %copy-start.11 = (f32[128]{0:T(128)S(1)}, f32[128]{0:T(128)}, u32[]{:S(2)}) copy-start(f32[128]{0:T(128)} %param.9) | copy-start | bytes 1540
  258.2 1.3 copy-start.4
  275.5 1.3 copy-start.5
  338.3 5.4 copy-start.2
  338.3 5.4 copy-start.3
  345.0 1.4 copy-start.6
  347.0 2.8 copy-start.8
  349.4 1.0 copy-start.7
  350.5 33.5 %copy-start.13 = (f32[2]{0:T(128)S(1)}, f32[2]{0:T(128)}, u32[]{:S(2)}) copy-start(f32[2]{0:T(128)} %constant.46) | copy-start | bytes 28
  382.6 125.3 %collective-permute-start.1 = (bf16[512,1024]{1,0:T(8,128)(2,1)}, bf16[512,1024]{1,0:T(8,128)(2,1)S(1)}, u32[]{:S(2)}, u32[]{:S(2)}) collective-permute-start(bf16[512,1024]{1,0:T(8,128)(2,1)} %fusion.26), channel_id=1, source_target_pairs={{0,1},{1,0},{2,3},{3,2},{4,5},{5,4},{6,7},{7,6},{8,9},{9,8},{10,11... | collective-permute-start | bytes 3145736 | tf_op jit(solution)/shard_map/ppermute | solution.py:89
  444.9 66.7 %collective-permute-start.2 = (bf16[512,1024]{1,0:T(8,128)(2,1)}, bf16[512,1024]{1,0:T(8,128)(2,1)}, u32[]{:S(2)}, u32[]{:S(2)}) collective-permute-start(bf16[512,1024]{1,0:T(8,128)(2,1)} %fusion.32), channel_id=1, source_target_pairs={{0,1},{1,0},{2,3},{3,2},{4,5},{5,4},{6,7},{7,6},{8,9},{9,8},{10,11... | collective-permute-start | bytes 3145736 | tf_op jit(solution)/shard_map/ppermute | solution.py:89
  502.5 9.2 %slice-start = ((s8[6291456]{0:T(1024)(128)(4,1)}), s8[4194304]{0:T(1024)(128)(4,1)S(1)}, s32[]{:S(2)}) async-start(s8[6291456]{0:T(1024)(128)(4,1)} %bitcast.41), calls=%async_computation.6 | async-start | bytes 8388608
  506.3 5.3 slice-start.1
  506.3 25.4 %collective-permute-start.3 = (bf16[512,1024]{1,0:T(8,128)(2,1)S(1)}, bf16[512,1024]{1,0:T(8,128)(2,1)S(1)}, u32[]{:S(2)}, u32[]{:S(2)}) collective-permute-start(bf16[512,1024]{1,0:T(8,128)(2,1)S(1)} %fusion.38), channel_id=1, source_target_pairs={{0,1},{1,0},{2,3},{3,2},{4,5},{5,4},{6,7},{7,6},{8,9},{9,8},{10,11... | collective-permute-start | bytes 3145736 | tf_op jit(solution)/shard_map/ppermute | solution.py:89
  511.6 20.1 %slice-start.2 = ((s8[6291456]{0:T(1024)(128)(4,1)}), s8[4194304]{0:T(1024)(128)(4,1)S(1)}, s32[]{:S(2)}) async-start(s8[6291456]{0:T(1024)(128)(4,1)} %bitcast.43), calls=%async_computation.8 | async-start | bytes 8388608
  511.6 20.1 %slice-start.3 = ((s8[6291456]{0:T(1024)(128)(4,1)}), s8[2097152]{0:T(1024)(128)(4,1)S(1)}, s32[]{:S(2)}) async-start(s8[6291456]{0:T(1024)(128)(4,1)} %bitcast.43), calls=%async_computation.9 | async-start | bytes 4194304
  534.8 1.7 copy-start.9
Sparse Core Ops, SparseCore 0:
  11.2 102.4 all-gather.8
  115.3 98.7 all-gather.10
  215.6 98.7 all-gather.6
  316.5 61.3 all-gather.12
  380.0 60.0 all-gather.14
  442.3 60.0 all-gather.16
where the time goes:
time: 548 us; the launch traced here: 544 us
  waiting for transfers between devices  246 us (45%)
  blocking collectives  98.2 us (18%)
  matrix products  89.1 us (16%)
  local copies, waits for them, and re-layouts  50.6 us (9%)
  other arithmetic  36.9 us (7%)
  between operations  14.9 us (3%)
  starting transfers between devices  7.74 us (1%)
    all_gather x3, waiting for transfers between devices, shards(): out_pieces.append(lax.all_gather(part, 'rep', axis=0, tiled=True))  139 us
    psum x1, blocking collectives, shards(): totals = lax.psum(jnp.stack([local_in, local_out]), ('rep', 'tp'))  98.2 us
    all_gather x3, waiting for transfers between devices, shards(): pieces.append(lax.all_gather(part, 'rep', axis=0, tiled=True))  89.7 us
    dot_general x3, matrix products, shards(): projected = jnp.dot(normed, piece, preferred_element_type=jnp.float32)  50.8 us
    unnamed x73, local copies, waits for them, and re-layouts  22.8 us
    dot_general x6, matrix products, product(): lax.dot_general(mixed, rows, (((1,), (1,)), ((), ())), preferred_element_...  22 us
    ppermute x3, waiting for transfers between devices, shards(): arrived = lax.ppermute(sent, 'tp', swap)  16.8 us
    reduce_sum x6, other arithmetic, layer_norm(): variance = jnp.mean(centred * centred, -1, keepdims=True)  14.3 us
  transfers between devices with their start and end apart: 10, of which 6 were waited for; matrix products, arithmetic and copies ran while one was open for 30% of the time, Pallas kernels for 0%

commit v1 on v0

--- a/solution.py
+++ b/solution.py
@@ -59,7 +59,9 @@
         out_pieces.append(lax.all_gather(part, "rep", axis=0, tiled=True))
     local_in = jnp.sum(jnp.square(project_in.astype(jnp.float32)))
     local_out = jnp.sum(jnp.square(project_out.astype(jnp.float32)))
-    totals = lax.psum(jnp.stack([local_in, local_out]), ("rep", "tp"))
+    totals = jnp.stack([local_in, local_out])
+    for name in ("tp", "rep"):
+        totals = lax.psum(totals, name)
     if n_tp == 2:
         other = lax.ppermute(activations, "tp", swap)
         other, totals = lax.optimization_barrier((other, totals))

time: 548 us -> 553 us (level)
    psum x1 -> x2, blocking collectives: 98.2 us -> 95.9 us  [shards(): totals = lax.psum(totals, name)]
where the time goes in v1:
time: 553 us; the launch traced here: 543 us
  waiting for transfers between devices  248 us (45%)
  blocking collectives  95.9 us (17%)
  matrix products  89.1 us (16%)
  local copies, waits for them, and re-layouts  50.6 us (9%)
  other arithmetic  36.9 us (7%)
  between operations  14.9 us (3%)
  starting transfers between devices  7.75 us (1%)
    all_gather x3, waiting for transfers between devices, shards(): out_pieces.append(lax.all_gather(part, 'rep', axis=0, tiled=True))  139 us
    psum x2, blocking collectives, shards(): totals = lax.psum(totals, name)  95.9 us
    all_gather x3, waiting for transfers between devices, shards(): pieces.append(lax.all_gather(part, 'rep', axis=0, tiled=True))  91.6 us
    dot_general x3, matrix products, shards(): projected = jnp.dot(normed, piece, preferred_element_type=jnp.float32)  50.8 us
    unnamed x73, local copies, waits for them, and re-layouts  22.7 us
    dot_general x6, matrix products, product(): lax.dot_general(mixed, rows, (((1,), (1,)), ((), ())), preferred_element_...  22 us
    ppermute x3, waiting for transfers between devices, shards(): arrived = lax.ppermute(sent, 'tp', swap)  16.8 us
    reduce_sum x6, other arithmetic, layer_norm(): variance = jnp.mean(centred * centred, -1, keepdims=True)  14.3 us
  transfers between devices with their start and end apart: 10, of which 6 were waited for; matrix products, arithmetic and copies ran while one was open for 30% of the time, Pallas kernels for 0%

profile of v1, /device:TPU:0, one launch (start us, length us, event | category | flops | bytes accessed | tf_op | source)
XLA Modules:
  0.0 543.2 jit_solution(18231373607069116772)
XLA Ops:
  7.2 2.4 fusion.113
  9.6 1.5 copy.45
  11.2 1.5 copy.48
  12.7 1.5 copy.42
  14.3 2.4 fusion.114
  17.4 3.0 collective-permute-start
  20.4 2.6 multiply_reduce_fusion.1
  23.0 2.4 multiply_reduce_fusion
  25.4 1.4 pad_maximum_fusion.1
  26.8 62.1 %psum.14 = f32[2]{0:T(128)S(1)} all-reduce(f32[2]{0:T(128)S(1)} %pad_maximum_fusion.1), channel_id=1, replica_groups=mesh['rep'=16,'tp'=2] {'tp'}, use_global_device_ids=true, to_apply=%region_2.0 | all-reduce | flops 2 | bytes 16 | tf_op jit(solution)/shard_map/psum | solution.py:64
  88.9 33.8 %psum.15 = f32[2]{0:T(128)S(1)} all-reduce(f32[2]{0:T(128)S(1)} %psum.14), channel_id=1, replica_groups=mesh['rep'=16,'tp'=2] {'rep'}, use_global_device_ids=true, to_apply=%region_3.0 | all-reduce | flops 2 | bytes 16 | tf_op jit(solution)/shard_map/psum | solution.py:64
  122.7 3.3 broadcast_select_fusion.1
  125.9 0.9 convert_reduce_fusion
  127.6 4.1 fusion.5
  131.8 17.0 %fusion.109 = f32[512,1536]{1,0:T(8,128)} fusion(bf16[6144,1536]{0,1:T(8,128)(2,1)} %all-gather.9.cloned.1.call-done, f32[6144]{0:T(1024)S(1)} %copy-done.12, f32[512]{0:T(512)S(1)} %add_rsqrt_fusion.6, f32[512]{0:T(512)S(1)} %broadcast_multiply_fusion.6, bf16[512,3072]{1,0:T(8,128)(2,1)} %copy-done, bf16[512,3072]{1,0:T(8,128)(2,1)S(1)} %get-tuple-element.12), kind=kOutput, calls=%fused_computation.164 | convolution fusion | flops 9688842240 | bytes 28340224 | tf_op jit(solution)/shard_map/dot_general | solution.py:76
  148.8 4.8 reshape.128
  153.6 60.0 %all-gather.11.cloned.1.call-done = bf16[6144,1536]{0,1:T(8,128)(2,1)} async-done(((bf16[384,1536]{0,1:T(8,128)(2,1)}), bf16[6144,1536]{0,1:T(8,128)(2,1)}) %all-gather.11.cloned.1.call-update) | async-done | bytes 18874384 | tf_op jit(solution)/shard_map/all_gather | solution.py:52
  213.6 17.2 %fusion.107 = f32[512,1536]{1,0:T(8,128)} fusion(bf16[6144,1536]{0,1:T(8,128)(2,1)} %all-gather.11.cloned.1.call-done, f32[6144]{0:T(1024)S(1)} %copy-done.12, f32[512]{0:T(512)S(1)} %add_rsqrt_fusion.6, f32[512]{0:T(512)S(1)} %broadcast_multiply_fusion.6, bf16[512,3072]{1,0:T(8,128)(2,1)} %copy-done, bf16[512,3072]{1,0:T(8,128)(2,1)S(1)} %get-tuple-element.12), kind=kOutput, calls=%fused_computation.163 | convolution fusion | flops 9688842240 | bytes 28340224 | tf_op jit(solution)/shard_map/dot_general | solution.py:76
  230.8 4.9 reshape.131
  235.7 6.6 %slice_reduce_fusion.1 = (f32[2,256,4]{2,1,0:T(8,128)}, f32[2,256,4]{2,1,0:T(8,128)}, f32[2,256,4,128]{3,2,1,0:T(4,128)}, f32[2,256,4,128]{3,2,1,0:T(4,128)}, f3...) fusion(f32[2,256,4,384]{3,2,1,0:T(4,128)} %reshape.131, ...), kind=kLoop, calls=%fused_computation.158 | loop fusion | flops 1040384 | bytes 8421376 | tf_op jit(solution)/shard_map/reduce_sum | solution.py:15
  242.3 2.2 slice.165
  244.6 2.2 slice.162
  246.7 1.1 copy.55
  247.8 1.1 copy.56
  248.9 2.1 copy.59
  251.0 1.9 multiply_reduce_fusion.6
  252.8 1.9 multiply_reduce_fusion.5
  254.8 2.9 fusion.55
  257.7 1.3 copy-done.4
  259.6 3.5 fusion.49
  263.0 2.1 copy.38
  265.2 1.1 copy.53
  266.3 2.1 copy.58
  268.4 1.9 multiply_reduce_fusion.8
  270.3 1.9 multiply_reduce_fusion.7
  272.2 2.7 fusion.54
  275.0 1.3 copy-done.5
  276.8 3.4 fusion.48
  280.2 2.1 copy.32
  282.3 31.6 %all-gather.7.cloned.1.call-done = bf16[6144,1536]{0,1:T(8,128)(2,1)} async-done(((bf16[384,1536]{0,1:T(8,128)(2,1)}), bf16[6144,1536]{0,1:T(8,128)(2,1)}) %all-gather.7.cloned.1.call-update) | async-done | bytes 18874384 | tf_op jit(solution)/shard_map/all_gather | solution.py:52
  313.9 16.6 %fusion.111 = f32[512,1536]{1,0:T(8,128)} fusion(bf16[6144,1536]{0,1:T(8,128)(2,1)} %all-gather.7.cloned.1.call-done, f32[6144]{0:T(1024)S(1)} %copy-done.12, f32[512]{0:T(512)S(1)} %add_rsqrt_fusion.6, f32[512]{0:T(512)S(1)} %broadcast_multiply_fusion.6, bf16[512,3072]{1,0:T(8,128)(2,1)} %copy-done, bf16[512,3072]{1,0:T(8,128)(2,1)S(1)} %get-tuple-element.12), kind=kOutput, calls=%fused_computation.165 | convolution fusion | flops 9688842240 | bytes 28340224 | tf_op jit(solution)/shard_map/dot_general | solution.py:76
  330.6 3.2 reshape.125
  333.8 1.0 slice.159
  334.8 3.1 slice_reduce_fusion.5
  337.9 1.2 copy.52
  339.2 1.3 copy.57
  340.5 2.7 multiply_reduce_fusion.9
  343.3 1.3 fusion.53
  344.6 1.3 copy-done.6
  346.5 2.4 fusion.47
  350.1 27.4 %all-gather.13.cloned.1.call-done = bf16[2048,1536]{1,0:T(8,128)(2,1)} async-done(((bf16[128,1536]{1,0:T(8,128)(2,1)}), bf16[2048,1536]{1,0:T(8,128)(2,1)}) %all-gather.13.cloned.1.call-update) | async-done | bytes 6291472 | tf_op jit(solution)/shard_map/all_gather | solution.py:59
  377.5 4.7 fusion.26
  382.2 1.5 collective-permute-start.1
  384.2 55.6 %all-gather.15.cloned.1.call-done = bf16[2048,1536]{1,0:T(8,128)(2,1)} async-done(((bf16[128,1536]{1,0:T(8,128)(2,1)}), bf16[2048,1536]{1,0:T(8,128)(2,1)}) %all-gather.15.cloned.1.call-update) | async-done | bytes 6291472 | tf_op jit(solution)/shard_map/all_gather | solution.py:59
  439.8 4.7 fusion.32
  444.5 1.5 collective-permute-start.2
  446.0 56.1 %all-gather.17.cloned.1.call-done = bf16[2048,1536]{1,0:T(8,128)(2,1)} async-done(((bf16[128,1536]{1,0:T(8,128)(2,1)}), bf16[2048,1536]{1,0:T(8,128)(2,1)}) %all-gather.17.cloned.1.call-update) | async-done | bytes 6291472 | tf_op jit(solution)/shard_map/all_gather | solution.py:59
  502.0 3.9 fusion.38
  505.9 1.5 collective-permute-start.3
  507.4 3.7 add_convert_fusion.2
  511.3 3.2 add_convert_fusion.1
  514.5 16.7 %collective-permute-done.3 = bf16[512,1024]{1,0:T(8,128)(2,1)S(1)} collective-permute-done((bf16[512,1024]{1,0:T(8,128)(2,1)S(1)}, bf16[512,1024]{1,0:T(8,128)(2,1)S(1)}, u32[]{:S(2)}, u32[]{:S(2)}) %collective-permute-start.3) | collective-permute-done | bytes 1048608 | tf_op jit(solution)/shard_map/ppermute | solution.py:91
  531.3 1.8 add_convert_fusion
  534.4 1.7 copy-done.9
  (98 shorter events, 6.5 us)
Async XLA Ops:
  7.2 124.6 %all-gather.9.cloned.1.call-start = ((), (), s32[]{:S(2)}) async-start(), calls=%async_computation.1 | async-start | bytes 20054016 | tf_op jit(solution)/shard_map/all_gather | solution.py:52
  11.1 202.5 %all-gather.11.cloned.1.call-start = ((), (), s32[]{:S(2)}) async-start(), calls=%async_computation.2 | async-start | bytes 20054016 | tf_op jit(solution)/shard_map/all_gather | solution.py:52
  12.7 301.3 %all-gather.7.cloned.1.call-start = ((), (), s32[]{:S(2)}) async-start(), calls=%async_computation | async-start | bytes 20054016 | tf_op jit(solution)/shard_map/all_gather | solution.py:52
  14.2 8.8 %copy-start.1 = (bf16[384,12,384]{2,0,1:T(8,128)(2,1)S(1)}, bf16[384,12,384]{2,0,1:T(8,128)(2,1)}, u32[]{:S(2)}) copy-start(bf16[384,12,384]{2,0,1:T(8,128)(2,1)} %param.11) | copy-start | bytes 10616836
  14.2 363.3 %all-gather.13.cloned.1.call-start = ((), (), s32[]{:S(2)}) async-start(), calls=%async_computation.3 | async-start | bytes 6684672 | tf_op jit(solution)/shard_map/all_gather | solution.py:59
  16.7 423.0 %all-gather.15.cloned.1.call-start = ((), (), s32[]{:S(2)}) async-start(), calls=%async_computation.4 | async-start | bytes 6684672 | tf_op jit(solution)/shard_map/all_gather | solution.py:59
  17.3 484.7 %all-gather.17.cloned.1.call-start = ((), (), s32[]{:S(2)}) async-start(), calls=%async_computation.5 | async-start | bytes 6684672 | tf_op jit(solution)/shard_map/all_gather | solution.py:59
  17.4 105.3 %collective-permute-start = (bf16[512,3072]{1,0:T(8,128)(2,1)}, bf16[512,3072]{1,0:T(8,128)(2,1)}, u32[]{:S(2)}, u32[]{:S(2)}) collective-permute-start(bf16[512,3072]{1,0:T(8,128)(2,1)} %param.7), channel_id=1, source_target_pairs={{0,1},{1,0},{2,3},{3,2},{4,5},{5,4},{6,7},{7,6},{8,9},{9,8},{10,11... | collective-permute-start | bytes 9437192 | tf_op jit(solution)/shard_map/ppermute | solution.py:66
  125.9 1.7 copy-start
  127.6 4.2 copy-start.12
  242.3 12.4 %copy-start.10 = (f32[128]{0:T(128)S(1)}, f32[128]{0:T(128)}, u32[]{:S(2)}) copy-start(f32[128]{0:T(128)} %param.10) | copy-start | bytes 1540
  242.3 12.5 %copy-start.11 = (f32[128]{0:T(128)S(1)}, f32[128]{0:T(128)}, u32[]{:S(2)}) copy-start(f32[128]{0:T(128)} %param.9) | copy-start | bytes 1540
  257.7 1.3 copy-start.4
  275.0 1.3 copy-start.5
  337.9 5.4 copy-start.2
  337.9 5.4 copy-start.3
  344.6 1.4 copy-start.6
  346.5 2.8 copy-start.8
  349.0 1.0 copy-start.7
  350.1 33.6 %copy-start.13 = (f32[2]{0:T(128)S(1)}, f32[2]{0:T(128)}, u32[]{:S(2)}) copy-start(f32[2]{0:T(128)} %constant.46) | copy-start | bytes 28
  382.2 125.3 %collective-permute-start.1 = (bf16[512,1024]{1,0:T(8,128)(2,1)}, bf16[512,1024]{1,0:T(8,128)(2,1)S(1)}, u32[]{:S(2)}, u32[]{:S(2)}) collective-permute-start(bf16[512,1024]{1,0:T(8,128)(2,1)} %fusion.26), channel_id=1, source_target_pairs={{0,1},{1,0},{2,3},{3,2},{4,5},{5,4},{6,7},{7,6},{8,9},{9,8},{10,11... | collective-permute-start | bytes 3145736 | tf_op jit(solution)/shard_map/ppermute | solution.py:91
  444.5 66.7 %collective-permute-start.2 = (bf16[512,1024]{1,0:T(8,128)(2,1)}, bf16[512,1024]{1,0:T(8,128)(2,1)}, u32[]{:S(2)}, u32[]{:S(2)}) collective-permute-start(bf16[512,1024]{1,0:T(8,128)(2,1)} %fusion.32), channel_id=1, source_target_pairs={{0,1},{1,0},{2,3},{3,2},{4,5},{5,4},{6,7},{7,6},{8,9},{9,8},{10,11... | collective-permute-start | bytes 3145736 | tf_op jit(solution)/shard_map/ppermute | solution.py:91
  502.0 9.2 %slice-start = ((s8[6291456]{0:T(1024)(128)(4,1)}), s8[4194304]{0:T(1024)(128)(4,1)S(1)}, s32[]{:S(2)}) async-start(s8[6291456]{0:T(1024)(128)(4,1)} %bitcast.41), calls=%async_computation.6 | async-start | bytes 8388608
  505.9 5.3 slice-start.1
  505.9 25.4 %collective-permute-start.3 = (bf16[512,1024]{1,0:T(8,128)(2,1)S(1)}, bf16[512,1024]{1,0:T(8,128)(2,1)S(1)}, u32[]{:S(2)}, u32[]{:S(2)}) collective-permute-start(bf16[512,1024]{1,0:T(8,128)(2,1)S(1)} %fusion.38), channel_id=1, source_target_pairs={{0,1},{1,0},{2,3},{3,2},{4,5},{5,4},{6,7},{7,6},{8,9},{9,8},{10,11... | collective-permute-start | bytes 3145736 | tf_op jit(solution)/shard_map/ppermute | solution.py:91
  511.2 20.1 %slice-start.2 = ((s8[6291456]{0:T(1024)(128)(4,1)}), s8[4194304]{0:T(1024)(128)(4,1)S(1)}, s32[]{:S(2)}) async-start(s8[6291456]{0:T(1024)(128)(4,1)} %bitcast.43), calls=%async_computation.8 | async-start | bytes 8388608
  511.2 20.1 %slice-start.3 = ((s8[6291456]{0:T(1024)(128)(4,1)}), s8[2097152]{0:T(1024)(128)(4,1)S(1)}, s32[]{:S(2)}) async-start(s8[6291456]{0:T(1024)(128)(4,1)} %bitcast.43), calls=%async_computation.9 | async-start | bytes 4194304
  534.4 1.7 copy-start.9
Sparse Core Ops, SparseCore 0:
  11.2 101.7 all-gather.8
  114.6 98.9 all-gather.10
  215.2 98.7 all-gather.6
  316.1 61.3 all-gather.12
  379.6 60.0 all-gather.14
  441.9 60.0 all-gather.16
